TPU v7x, 32 devices: a whole 2x2x4 slice. The times are simulated.
32 devices in a mesh: dp: 8 (over z, core), tensor: 4 (over y, x).
Axes of the slice: x: 2, y: 2, z: 4, core: 2. Of those that a mesh axis runs over, the one named last changes fastest.
Arguments:
- latents: bfloat16 [88, 256, 640], P('dp', 'tensor'), may hold values from -6 to 6
- cotangent: bfloat16 [88, 256, 640], P('dp', 'tensor'), may hold values from -6 to 6
- trunc_steps: int32 [8], replicated, may hold values from 30 to 40, as said below
- timesteps: int32 [88], replicated, may hold values from 100 to 900
- tile_map: int32 [88], replicated, may hold values from 0 to 87, as said below
- gain: float32 [640], replicated, may hold values from 0.5 to 1.5
- w_value: bfloat16 [640, 2560], P(None, 'tensor'), may hold values from -0.25 to 0.25
- w_gate: bfloat16 [640, 2560], P(None, 'tensor'), may hold values from -0.25 to 0.25
- w_out: bfloat16 [640, 2560], P(None, 'tensor'), may hold values from -0.125 to 0.125
Outputs:
- placed_grad: bfloat16 [88, 256, 640], P('dp', 'tensor')
- grad_value: float32 [640, 2560], P('dp', 'tensor')
- grad_gate: float32 [640, 2560], P('dp', 'tensor')
- grad_out_proj: float32 [640, 2560], P('dp', 'tensor')
- grad_gain: float32 [640], replicated
Inputs may be any that keep to these rules, and one draw needn't show every extreme that they name: trunc_steps lies in 30 to 40, so a prompt has 1 to 11 live slots, its lowest ones. tile_map is a permutation of 0 to 87. Output slots g * 11 to g * 11 + 10 form group g; the live items go to the lowest slots of the groups, and each group receives the floor or the ceiling of (number of live items) / 8 of them.
All inputs are finite; a program needn't handle non-finite values.
Results may differ from a plain program's by a relative error of at most 0.0068.
Values may be sent and summed in bfloat16 or wider, within the bound.
A program may use at most 64 MiB of HBM per device.

v0:
```python
import jax
import jax.numpy as jnp
from jax import lax
from jax.sharding import PartitionSpec as P

eps = 1e-05


def alpha_bars():
    betas = jnp.linspace(0.00085**0.5, 0.012**0.5, 1000, dtype=jnp.float32) ** 2
    return jnp.exp(jnp.cumsum(jnp.log1p(-betas)))


def gelu_parts(inputs):
    cdf = 0.5 * (1.0 + lax.erf(inputs * 0.7071067811865476))
    density = jnp.exp(-0.5 * inputs * inputs) * 0.3989422804014327
    return (inputs * cdf, cdf + inputs * density)


def norm_backward(d_normed, grad_part, hat_part, inv_part, gain):
    d_hat = d_normed * gain
    input_grad = grad_part.astype(jnp.float32) + inv_part * (
        d_hat
        - jnp.mean(d_hat, axis=-1, keepdims=True)
        - hat_part * jnp.mean(d_hat * hat_part, axis=-1, keepdims=True)
    )
    gain_local = jnp.sum(d_normed * hat_part, axis=(0, 1))
    return (input_grad, gain_local)


def tile_backward(tiles, cot_tiles, slot_times, live_count, gain, w_value, w_gate, w_out):
    full_x, full_cot = (
        lax.all_gather(tiles, "tensor", axis=1, tiled=True),
        lax.all_gather(cot_tiles, "tensor", axis=1, tiled=True),
    )
    width = full_x.shape[2]
    local_rows = tiles.shape[1]
    inner = w_value.shape[1]
    slot_total = full_x.shape[0]
    table = alpha_bars()
    picked = jnp.sum(
        jnp.where(
            slot_times[:, None] == jnp.arange(1000, dtype=jnp.int32)[None, :], table[None, :], 0.0
        ),
        axis=1,
    )
    noise_scale = jnp.sqrt(1.0 - picked)
    x_float = full_x.astype(jnp.float32)
    row_mean = jnp.mean(x_float, axis=-1, keepdims=True)
    centred = x_float - row_mean
    row_var = jnp.mean(centred * centred, axis=-1, keepdims=True)
    inv_std = lax.rsqrt(row_var + eps)
    x_hat = centred * inv_std
    normed = (x_hat * gain).astype(jnp.bfloat16)
    grad_tile = (full_cot.astype(jnp.float32) * noise_scale[:, None, None]).astype(jnp.bfloat16)
    first_dims = (((0,), (0,)), ((), ()))
    last_dims = (((1,), (1,)), ((), ()))

    def one_slot(slot_idx, carry):
        acc_wv, acc_wg, acc_wo, normed_buf = carry
        norm_tile = lax.dynamic_index_in_dim(normed, slot_idx, 0, keepdims=False)
        grad_one = lax.dynamic_index_in_dim(grad_tile, slot_idx, 0, keepdims=False)
        values_proj = jnp.dot(norm_tile, w_value, preferred_element_type=jnp.float32)
        gate_proj = jnp.dot(norm_tile, w_gate, preferred_element_type=jnp.float32)
        gelu_gate, gelu_slope = gelu_parts(gate_proj)
        hidden = (values_proj * gelu_gate).astype(jnp.bfloat16)
        d_hidden = jnp.dot(grad_one, w_out, preferred_element_type=jnp.float32)
        d_value = (d_hidden * gelu_gate).astype(jnp.bfloat16)
        d_gate = (d_hidden * values_proj * gelu_slope).astype(jnp.bfloat16)
        acc_wv = acc_wv + lax.dot_general(
            norm_tile, d_value, first_dims, preferred_element_type=jnp.float32
        )
        acc_wg = acc_wg + lax.dot_general(
            norm_tile, d_gate, first_dims, preferred_element_type=jnp.float32
        )
        acc_wo = acc_wo + lax.dot_general(
            grad_one, hidden, first_dims, preferred_element_type=jnp.float32
        )
        d_normed = lax.dot_general(d_value, w_value, last_dims, preferred_element_type=jnp.float32)
        d_normed = d_normed + lax.dot_general(
            d_gate, w_gate, last_dims, preferred_element_type=jnp.float32
        )
        normed_buf = lax.dynamic_update_index_in_dim(normed_buf, d_normed, slot_idx, 0)
        return (acc_wv, acc_wg, acc_wo, normed_buf)

    zero_w = jnp.zeros((width, inner), jnp.float32)
    init = (zero_w, zero_w, zero_w, jnp.zeros(full_x.shape, jnp.float32))
    acc_wv, acc_wg, acc_wo, normed_buf = lax.fori_loop(0, live_count, one_slot, init)
    offset = lax.axis_index("tensor") * local_rows
    hat_part = lax.dynamic_slice_in_dim(x_hat, offset, local_rows, 1)
    inv_part = lax.dynamic_slice_in_dim(inv_std, offset, local_rows, 1)
    grad_part = lax.dynamic_slice_in_dim(grad_tile, offset, local_rows, 1)
    slot_live = (jnp.arange(slot_total, dtype=jnp.int32) < live_count)[:, None, None]
    d_normed = lax.psum_scatter(normed_buf, "tensor", scatter_dimension=1, tiled=True)
    input_grad, gain_local = norm_backward(d_normed, grad_part, hat_part, inv_part, gain)
    input_grad = jnp.where(slot_live, input_grad, 0.0).astype(jnp.bfloat16)
    return (input_grad, (acc_wv, acc_wg, acc_wo), gain_local)


def per_device(latents, cotangent, trunc_steps, timesteps, tile_map, gain, w_value, w_gate, w_out):
    slot_total = latents.shape[0]
    total = tile_map.shape[0]
    my_group = lax.axis_index("dp")
    item_ids = jnp.arange(total, dtype=jnp.int32)
    live_all = (item_ids % slot_total < jnp.repeat(trunc_steps, slot_total) - 29).astype(jnp.int32)
    my_slots = my_group * slot_total + jnp.arange(slot_total, dtype=jnp.int32)
    is_mine = tile_map[:, None] == my_slots[None, :]
    dest_source = jnp.sum(jnp.where(is_mine, item_ids[:, None], 0), axis=0)
    every_x, every_cot = (
        lax.all_gather(latents, "dp", axis=0, tiled=True),
        lax.all_gather(cotangent, "dp", axis=0, tiled=True),
    )
    tiles = jnp.take(every_x, dest_source, axis=0)
    cot_tiles = jnp.take(every_cot, dest_source, axis=0)
    slot_times = jnp.take(timesteps, dest_source)
    live_count = jnp.sum(jnp.take(live_all, dest_source))
    placed_grad, weight_parts, gain_local = tile_backward(
        tiles, cot_tiles, slot_times, live_count, gain, w_value, w_gate, w_out
    )
    grad_value, grad_gate, grad_out_proj = (
        lax.psum_scatter(weight_parts[0], "dp", scatter_dimension=0, tiled=True),
        lax.psum_scatter(weight_parts[1], "dp", scatter_dimension=0, tiled=True),
        lax.psum_scatter(weight_parts[2], "dp", scatter_dimension=0, tiled=True),
    )
    grad_gain = lax.psum(gain_local, ("dp", "tensor"))
    return (placed_grad, grad_value, grad_gate, grad_out_proj, grad_gain)


def solution(mesh):
    in_specs = (
        P("dp", "tensor", None),
        P("dp", "tensor", None),
        P(),
        P(),
        P(),
        P(),
        P(None, "tensor"),
        P(None, "tensor"),
        P(None, "tensor"),
    )
    out_specs = (
        P("dp", "tensor", None),
        P("dp", "tensor"),
        P("dp", "tensor"),
        P("dp", "tensor"),
        P(),
    )
    return jax.shard_map(
        per_device, mesh=mesh, in_specs=in_specs, out_specs=out_specs, check_vma=False
    )
```

profile of v0, /device:TPU:0, one launch (start us, length us, event | category | flops | bytes accessed | tf_op | source)
XLA Modules:
  0.0 554.6 jit_solution(17423337908804927241)
XLA Ops:
  10.3 74.4 %all-gather.9.cloned.1.call-done = bf16[88,64,640]{2,1,0:T(8,128)(2,1)} async-done(((bf16[11,64,640]{2,1,0:T(8,128)(2,1)}), bf16[88,64,640]{2,1,0:T(8,128)(2,1)}) %all-gather.9.cloned.1.call-update) | async-done | bytes 7208976 | tf_op jit(solution)/shard_map/all_gather | solution.py:110
  84.7 3.8 gather_fusion.3
  88.4 68.8 %all-gather.5.cloned.1.call-done = bf16[88,64,640]{2,1,0:T(8,128)(2,1)} async-done(((bf16[11,64,640]{2,1,0:T(8,128)(2,1)}), bf16[88,64,640]{2,1,0:T(8,128)(2,1)}) %all-gather.5.cloned.1.call-update) | async-done | bytes 7208976 | tf_op jit(solution)/shard_map/all_gather | solution.py:111
  157.2 3.8 gather_fusion.1
  165.5 43.4 %all-gather.11.cloned.1.call-done = bf16[11,256,640]{2,1,0:T(8,128)(2,1)} async-done(((bf16[11,64,640]{2,1,0:T(8,128)(2,1)}), bf16[11,256,640]{2,1,0:T(8,128)(2,1)}) %all-gather.11.cloned.1.call-update) | async-done | bytes 3604496 | tf_op jit(solution)/shard_map/all_gather | solution.py:33
  208.9 2.7 convert_reduce_fusion
  213.4 45.5 %all-gather.7.cloned.1.call-done = bf16[11,256,640]{2,1,0:T(8,128)(2,1)} async-done(((bf16[11,64,640]{2,1,0:T(8,128)(2,1)}), bf16[11,256,640]{2,1,0:T(8,128)(2,1)}) %all-gather.7.cloned.1.call-update) | async-done | bytes 3604496 | tf_op jit(solution)/shard_map/all_gather | solution.py:34
  258.9 5.0 multiply_convert_fusion.4
  263.9 4.8 fusion.32
  271.3 3.6 broadcast_in_dim.84
  274.9 88.8 %while.16 = (s32[]{:T(128)}, f32[640,640]{1,0:T(8,128)}, f32[640,640]{1,0:T(8,128)}, f32[640,640]{1,0:T(8,128)S(1)}, f32[11,256,640]{2,1,0:T(8,128)}, /*index=5*...) while((s32[]{:T(128)}, f32[640,640]{1,0:T(8,128)}, ...), condition=%wide.region_8.11_spmd, body=%wide.region_7.10_spmd.sunk | while | flops 1684684800 | bytes 56197460 | solution.py:88
  282.3 2.0 convolution_add_fusion.8
  284.2 1.9 convolution_add_fusion.9
  294.8 2.0 convolution_add_fusion.8
  296.8 1.9 convolution_add_fusion.9
  307.5 2.0 convolution_add_fusion.8
  309.5 1.9 convolution_add_fusion.9
  320.1 2.0 convolution_add_fusion.8
  322.1 1.9 convolution_add_fusion.9
  332.7 2.0 convolution_add_fusion.8
  334.7 1.9 convolution_add_fusion.9
  345.3 2.0 convolution_add_fusion.8
  347.3 1.9 convolution_add_fusion.9
  354.3 1.6 multiply_convert_fusion.8
  357.9 2.0 convolution_add_fusion.8
  359.9 1.9 convolution_add_fusion.9
  367.7 71.2 %reduce-scatter.5.cloned.1.call-done = f32[11,64,640]{2,1,0:T(8,128)} async-done(((f32[11,256,640]{2,1,0:T(8,128)}), f32[11,64,640]{2,1,0:T(8,128)}) %reduce-scatter.5.cloned.1.call-update) | async-done | bytes 1802256 | tf_op jit(solution)/shard_map/reduce_scatter | solution.py:94
  438.8 2.8 multiply_reduce_fusion
  441.6 39.6 %psum.7 = f32[640]{0:T(1024)} all-reduce(f32[640]{0:T(1024)S(1)} %get-tuple-element.72), channel_id=1, replica_groups=mesh['dp'=8,'tensor'=4] {'dp','tensor'}, use_global_device_ids=true, to_apply=%region_16.19 | all-reduce | flops 640 | bytes 5120 | tf_op jit(solution)/shard_map/psum | solution.py:125
  481.3 3.3 select_convert_fusion
  484.6 27.5 %reduce-scatter.9.cloned.1.call-done = f32[80,640]{1,0:T(8,128)} async-done(((f32[640,640]{1,0:T(8,128)}), f32[80,640]{1,0:T(8,128)}) %reduce-scatter.9.cloned.1.call-update) | async-done | bytes 204816 | tf_op jit(solution)/shard_map/reduce_scatter | solution.py:122
  512.1 35.7 %reduce-scatter.11.cloned.1.call-done = f32[80,640]{1,0:T(8,128)} async-done(((f32[640,640]{1,0:T(8,128)}), f32[80,640]{1,0:T(8,128)}) %reduce-scatter.11.cloned.1.call-update) | async-done | bytes 204816 | tf_op jit(solution)/shard_map/reduce_scatter | solution.py:123
  (179 shorter events, 70.9 us)
Async XLA Ops:
  7.2 77.5 %all-gather.9.cloned.1.call-start = ((), (), s32[]{:S(2)}) async-start(), calls=%async_computation.6 | async-start | bytes 8110080 | tf_op jit(solution)/shard_map/all_gather | solution.py:110
  7.9 149.3 %all-gather.5.cloned.1.call-start = ((), (), s32[]{:S(2)}) async-start(), calls=%async_computation.4 | async-start | bytes 8110080 | tf_op jit(solution)/shard_map/all_gather | solution.py:111
  8.7 200.2 %all-gather.11.cloned.1.call-start = ((), (), s32[]{:S(2)}) async-start(), calls=%async_computation.7 | async-start | bytes 4505600 | tf_op jit(solution)/shard_map/all_gather | solution.py:33
  88.4 74.7 %copy-start.13 = (s32[8]{0:T(128)S(1)}, s32[8]{0:T(128)}, u32[]{:S(2)}) copy-start(s32[8]{0:T(128)} %param.17) | copy-start | bytes 100
  162.5 96.4 %all-gather.7.cloned.1.call-start = ((), (), s32[]{:S(2)}) async-start(), calls=%async_computation.5 | async-start | bytes 4505600 | tf_op jit(solution)/shard_map/all_gather | solution.py:34
  163.1 275.8 %reduce-scatter.5.cloned.1.call-start = ((), (), s32[]{:S(2)}) async-start(), calls=%async_computation.8 | async-start | bytes 9011200 | tf_op jit(solution)/shard_map/reduce_scatter | solution.py:94
  213.4 50.5 %copy-start.12 = (f32[640]{0:T(1024)S(1)}, f32[640]{0:T(1024)}, u32[]{:S(2)}) copy-start(f32[640]{0:T(1024)} %param.20) | copy-start | bytes 7684
  258.9 5.0 copy-start.9
  271.3 3.6 copy-start.1
  271.3 3.6 copy-start.2
  277.1 3.6 copy-start.6
  278.6 3.6 copy-start.4
  282.2 3.9 copy-start.7
  289.6 3.6 copy-start.6
  291.2 3.6 copy-start.4
  294.8 3.9 copy-start.7
  302.3 3.6 copy-start.6
  307.5 3.9 copy-start.7
  314.9 3.6 copy-start.6
  316.5 3.6 copy-start.4
  320.1 3.9 copy-start.7
  327.5 3.6 copy-start.6
  332.7 3.9 copy-start.7
  340.1 3.6 copy-start.6
  341.7 3.6 copy-start.4
  345.3 3.9 copy-start.7
  352.7 3.6 copy-start.6
  357.9 3.9 copy-start.7
  364.9 119.6 %reduce-scatter.7.cloned.1.call-start = ((), (), s32[]{:S(2)}) async-start(), calls=%async_computation.9 | async-start | bytes 1843200 | tf_op jit(solution)/shard_map/reduce_scatter | solution.py:121
  365.5 146.6 %reduce-scatter.9.cloned.1.call-start = ((), (), s32[]{:S(2)}) async-start(), calls=%async_computation.10 | async-start | bytes 1843200 | tf_op jit(solution)/shard_map/reduce_scatter | solution.py:122
  366.3 181.5 %reduce-scatter.11.cloned.1.call-start = ((), (), s32[]{:S(2)}) async-start(), calls=%async_computation.11 | async-start | bytes 1843200 | tf_op jit(solution)/shard_map/reduce_scatter | solution.py:123
  438.8 42.4 %copy-start.11 = (f32[11,64,640]{2,1,0:T(8,128)S(1)}, f32[11,64,640]{2,1,0:T(8,128)}, u32[]{:S(2)}) copy-start(f32[11,64,640]{2,1,0:T(8,128)} %reduce-scatter.5.cloned.1.call-done) | copy-start | bytes 5406724
  (20 other events, 62.5 us)
Sparse Core Ops, SparseCore 0:
  9.6 74.9 all-gather.8
  86.3 70.8 all-gather.4
  162.6 46.2 all-gather.10
  211.2 47.6 all-gather.6
  363.9 74.8 reduce-scatter.4
  441.6 34.4 reduce-scatter.6
  479.0 33.0 reduce-scatter.8
  514.9 32.7 reduce-scatter.10
where the time goes:
time: 551 us; the launch traced here: 555 us
  waiting for transfers between devices  370 us (67%)
  matrix products  83.2 us (15%)
  blocking collectives  39.6 us (7%)
  other arithmetic  24.2 us (4%)
  local copies, waits for them, and re-layouts  17.3 us (3%)
  between operations  14.3 us (3%)
    all_gather x1, waiting for transfers between devices, per_device(): lax.all_gather(latents, 'dp', axis=0, tiled=True)  74.4 us
    reduce_scatter x1, waiting for transfers between devices, tile_backward(): lax.psum_scatter(normed_buf, 'tensor', scatter_dimension=1, tiled=True)  71.2 us
    all_gather x1, waiting for transfers between devices, per_device(): lax.all_gather(cotangent, 'dp', axis=0, tiled=True)  68.8 us
    all_gather x1, waiting for transfers between devices, tile_backward(): lax.all_gather(cot_tiles, 'tensor', axis=1, tiled=True)  45.5 us
    all_gather x1, waiting for transfers between devices, tile_backward(): lax.all_gather(tiles, 'tensor', axis=1, tiled=True)  43.4 us
    psum x1, blocking collectives, per_device(): grad_gain = lax.psum(gain_local, ('dp', 'tensor'))  39.6 us
    reduce_scatter x1, waiting for transfers between devices, per_device(): lax.psum_scatter(weight_parts[2], 'dp', scatter_dimension=0, tiled=True)  35.7 us
    reduce_scatter x1, waiting for transfers between devices, per_device(): lax.psum_scatter(weight_parts[1], 'dp', scatter_dimension=0, tiled=True)  27.5 us
  transfers between devices with their start and end apart: 8, of which 7 were waited for; matrix products, arithmetic and copies ran while one was open for 3% of the time, Pallas kernels for 0%

commit v1 on v0

v1 whole, which is shorter than its diff:
```python
import functools

import jax
import jax.numpy as jnp
import numpy as np
from jax import lax
from jax.experimental import pallas as pl
from jax.experimental.pallas import tpu as pltpu
from jax.sharding import PartitionSpec as P

eps = 1e-05


def noise_table():
    betas = np.linspace(0.00085**0.5, 0.012**0.5, 1000) ** 2
    abar = np.exp(np.cumsum(np.log1p(-betas)))
    return np.sqrt(1.0 - abar).astype(np.float32)


def block_kernel(live_ref, scale_ref, x_ref, cot_ref, gain_ref, wv_ref, wg_ref, wo_ref,
                 dn_ref, dw_ref, acc_v, acc_g, acc_o):
    step = pl.program_id(0)
    inner = wv_ref.shape[1]
    first = (((0,), (0,)), ((), ()))
    last = (((1,), (1,)), ((), ()))

    @pl.when(step == 0)
    def _():
        acc_v[...] = jnp.zeros_like(acc_v)
        acc_g[...] = jnp.zeros_like(acc_g)
        acc_o[...] = jnp.zeros_like(acc_o)

    @pl.when(step < live_ref[0])
    def _():
        x = x_ref[0].astype(jnp.float32)
        centred = x - jnp.mean(x, axis=-1, keepdims=True)
        inv_std = lax.rsqrt(jnp.mean(centred * centred, axis=-1, keepdims=True) + eps)
        normed = (centred * inv_std * gain_ref[...]).astype(jnp.bfloat16)
        grad = (cot_ref[0].astype(jnp.float32) * scale_ref[step]).astype(jnp.bfloat16)
        values = jnp.dot(normed, wv_ref[...], preferred_element_type=jnp.float32)
        gate = jnp.dot(normed, wg_ref[...], preferred_element_type=jnp.float32)
        d_hidden = jnp.dot(grad, wo_ref[...], preferred_element_type=jnp.float32)
        cdf = 0.5 * (1.0 + lax.erf(gate * 0.7071067811865476))
        density = jnp.exp(-0.5 * gate * gate) * 0.3989422804014327
        gelu = gate * cdf
        hidden = (values * gelu).astype(jnp.bfloat16)
        d_value = (d_hidden * gelu).astype(jnp.bfloat16)
        d_gate = (d_hidden * values * (cdf + gate * density)).astype(jnp.bfloat16)
        acc_v[...] += lax.dot_general(normed, d_value, first, preferred_element_type=jnp.float32)
        acc_g[...] += lax.dot_general(normed, d_gate, first, preferred_element_type=jnp.float32)
        acc_o[...] += lax.dot_general(grad, hidden, first, preferred_element_type=jnp.float32)
        d_normed = lax.dot_general(d_value, wv_ref[...], last, preferred_element_type=jnp.float32)
        d_normed += lax.dot_general(d_gate, wg_ref[...], last, preferred_element_type=jnp.float32)
        dn_ref[0] = d_normed.astype(jnp.bfloat16)

    @pl.when(step == pl.num_programs(0) - 1)
    def _():
        dw_ref[:, 0:inner] = acc_v[...].astype(jnp.bfloat16)
        dw_ref[:, inner : 2 * inner] = acc_g[...].astype(jnp.bfloat16)
        dw_ref[:, 2 * inner : 3 * inner] = acc_o[...].astype(jnp.bfloat16)


def block_backward(live, scale, x, cot, gain, w_value, w_gate, w_out):
    slots, rows, width = x.shape
    inner = w_value.shape[1]

    def tile(t, live_ref, scale_ref):
        return (jnp.minimum(t, live_ref[0] - 1), 0, 0)

    def whole(t, live_ref, scale_ref):
        return (0, 0)

    weight = pl.BlockSpec((width, inner), whole)
    return pl.pallas_call(
        block_kernel,
        grid_spec=pltpu.PrefetchScalarGridSpec(
            num_scalar_prefetch=2,
            grid=(slots,),
            in_specs=[
                pl.BlockSpec((1, rows, width), tile),
                pl.BlockSpec((1, rows, width), tile),
                pl.BlockSpec((1, width), whole),
                weight,
                weight,
                weight,
            ],
            out_specs=[
                pl.BlockSpec((1, rows, width), tile),
                pl.BlockSpec((width, 3 * inner), whole),
            ],
            scratch_shapes=[pltpu.VMEM((width, inner), jnp.float32)] * 3,
        ),
        out_shape=[
            jax.ShapeDtypeStruct((slots, rows, width), jnp.bfloat16),
            jax.ShapeDtypeStruct((width, 3 * inner), jnp.bfloat16),
        ],
        compiler_params=pltpu.CompilerParams(
            dimension_semantics=("arbitrary",), vmem_limit_bytes=48 * 1024 * 1024
        ),
    )(live, scale, x, cot, gain, w_value, w_gate, w_out)


def per_device(latents, cotangent, trunc_steps, timesteps, tile_map, gain, w_value, w_gate, w_out):
    slots, local_rows, width = latents.shape
    total = tile_map.shape[0]
    inner = w_value.shape[1]
    me = lax.axis_index("dp")
    live = jnp.clip(lax.dynamic_index_in_dim(trunc_steps, me, 0, keepdims=True) - 29, 1, slots)
    times = lax.dynamic_slice_in_dim(timesteps, me * slots, slots, 0)
    table = jnp.asarray(noise_table())
    scale = jnp.sum(
        jnp.where(times[:, None] == jnp.arange(1000, dtype=jnp.int32)[None, :], table[None, :], 0.0),
        axis=1,
    )
    full_x = lax.all_gather(latents, "tensor", axis=1, tiled=True)
    full_cot = lax.all_gather(cotangent, "tensor", axis=1, tiled=True)
    dn_part, dw_part = block_backward(
        live, scale, full_x, full_cot, gain[None, :], w_value, w_gate, w_out
    )
    d_normed = lax.psum_scatter(dn_part, "tensor", scatter_dimension=1, tiled=True)
    dw = lax.psum_scatter(dw_part, "dp", scatter_dimension=0, tiled=True).astype(jnp.float32)

    slot_live = (jnp.arange(slots, dtype=jnp.int32) < live[0])[:, None, None]
    d_normed = jnp.where(slot_live, d_normed.astype(jnp.float32), 0.0)
    x = latents.astype(jnp.float32)
    centred = x - jnp.mean(x, axis=-1, keepdims=True)
    inv_std = lax.rsqrt(jnp.mean(centred * centred, axis=-1, keepdims=True) + eps)
    x_hat = centred * inv_std
    grad = (cotangent.astype(jnp.float32) * scale[:, None, None]).astype(jnp.bfloat16)
    d_hat = d_normed * gain
    input_grad = grad.astype(jnp.float32) + inv_std * (
        d_hat
        - jnp.mean(d_hat, axis=-1, keepdims=True)
        - x_hat * jnp.mean(d_hat * x_hat, axis=-1, keepdims=True)
    )
    input_grad = jnp.where(slot_live, input_grad, 0.0).astype(jnp.bfloat16)
    grad_gain = lax.psum(jnp.sum(d_normed * x_hat, axis=(0, 1)), ("dp", "tensor"))

    item_ids = jnp.arange(total, dtype=jnp.int32)
    source = jnp.sum(
        jnp.where(tile_map[:, None] == item_ids[None, :], item_ids[:, None], 0), axis=0
    )
    pieces = lax.all_to_all(input_grad, "dp", split_axis=1, concat_axis=0, tiled=True)
    pieces = jnp.take(pieces, source, axis=0)
    placed = lax.all_to_all(pieces, "dp", split_axis=0, concat_axis=1, tiled=True)
    return (
        placed,
        dw[:, :inner],
        dw[:, inner : 2 * inner],
        dw[:, 2 * inner :],
        grad_gain,
    )


def solution(mesh):
    in_specs = (
        P("dp", "tensor", None),
        P("dp", "tensor", None),
        P(),
        P(),
        P(),
        P(),
        P(None, "tensor"),
        P(None, "tensor"),
        P(None, "tensor"),
    )
    out_specs = (
        P("dp", "tensor", None),
        P("dp", "tensor"),
        P("dp", "tensor"),
        P("dp", "tensor"),
        P(),
    )
    return jax.shard_map(
        per_device, mesh=mesh, in_specs=in_specs, out_specs=out_specs, check_vma=False
    )
```

time: 551 us -> 308 us (0.56)
  waiting for transfers between devices: 370 us -> 217 us
  matrix products: 83.2 us -> 0 us
  other arithmetic: 24.2 us -> 5.28 us
  Pallas kernels: 0 us -> 15.5 us
  local copies, waits for them, and re-layouts: 17.3 us -> 7.81 us
  starting transfers between devices: 0.27 us -> 8.44 us
    all_gather x4 -> x2, waiting for transfers between devices: 232 us -> 99.5 us  [the longest x1 50 us: per_device(): full_x = lax.all_gather(latents, 'tensor', axis=1, tiled=True)]
    dot_general x56 -> x0, matrix products: 83.2 us -> none  [the longest x7 13.7 us: one_slot(): lax.dot_general(norm_tile, d_gate, first_dims, preferred_element_type=jnp...]
    reduce_scatter x4 -> x2, waiting for transfers between devices: 134 us -> 65.5 us  [the longest x1 65.5 us: per_device(): lax.psum_scatter(dn_part, 'tensor', scatter_dimension=1, tiled=True)]
    all_to_all x0 -> x2, waiting for transfers between devices: none -> 49.8 us  [the longest x1 49.8 us: per_device(): lax.all_to_all(input_grad, 'dp', split_axis=1, concat_axis=0, tiled=True)]
    pallas_call x0 -> x1, Pallas kernels: none -> 15.5 us  [block_backward(): pl.pallas_call(block_kernel, grid_spec=pltpu.PrefetchScalarGridSpec(num_s...]
    all_to_all x0 -> x2, starting transfers between devices: none -> 8.28 us  [the longest x1 4.73 us: per_device(): lax.all_to_all(input_grad, 'dp', split_axis=1, concat_axis=0, tiled=True)]
    gather x4 -> x1, local copies, waits for them, and re-layouts: 8.83 us -> 0.74 us  [per_device(): pieces = jnp.take(pieces, source, axis=0)]
    convert_element_type x3 -> x1, other arithmetic: 8.3 us -> 1.03 us  [per_device(): input_grad = jnp.where(slot_live, input_grad, 0.0).astype(jnp.bfloat16)]
  transfers between devices with their start and end apart: 8 -> 6, of which waited for: 7 -> 4; matrix products, arithmetic and copies ran while one was open for 3% -> 3% of each run, Pallas kernels for 0% -> 0%
where the time goes in v1:
time: 308 us; the launch traced here: 310 us
  waiting for transfers between devices  217 us (70%)
  blocking collectives  41.2 us (13%)
  Pallas kernels  15.5 us (5%)
  between operations  14.6 us (5%)
  starting transfers between devices  8.44 us (3%)
  local copies, waits for them, and re-layouts  7.81 us (3%)
  other arithmetic  5.28 us (2%)
    reduce_scatter x1, waiting for transfers between devices, per_device(): lax.psum_scatter(dn_part, 'tensor', scatter_dimension=1, tiled=True)  65.5 us
    all_gather x1, waiting for transfers between devices, per_device(): full_x = lax.all_gather(latents, 'tensor', axis=1, tiled=True)  50 us
    all_to_all x1, waiting for transfers between devices, per_device(): lax.all_to_all(input_grad, 'dp', split_axis=1, concat_axis=0, tiled=True)  49.8 us
    all_gather x1, waiting for transfers between devices, per_device(): full_cot = lax.all_gather(cotangent, 'tensor', axis=1, tiled=True)  49.5 us
    psum x1, blocking collectives, per_device(): lax.psum(jnp.sum(d_normed * x_hat, axis=(0, 1)), ('dp', 'tensor'))  41.2 us
    pallas_call x1, Pallas kernels, block_backward(): pl.pallas_call(block_kernel, grid_spec=pltpu.PrefetchScalarGridSpec(num_s...  15.5 us
  transfers between devices with their start and end apart: 6, of which 4 were waited for; matrix products, arithmetic and copies ran while one was open for 3% of the time, Pallas kernels for 0%

profile of v1, /device:TPU:0, one launch (start us, length us, event | category | flops | bytes accessed | tf_op | source)
XLA Modules:
  0.0 309.7 jit_solution(6573579496934523812)
XLA Ops:
  7.2 0.0 all-gather.3.cloned.1.call-start
  7.3 0.7 all-gather.3.cloned.1.call-update
  8.0 0.0 all-gather.5.cloned.1.call-start
  8.0 0.7 all-gather.5.cloned.1.call-update
  8.7 0.0 reduce-scatter.3.cloned.1.call-start
  8.8 0.1 dynamic_slice.8
  8.9 0.6 dynamic_slice.7
  10.1 0.2 select_reduce_fusion.scale_ref
  10.3 50.0 %all-gather.3.cloned.1.call-done.x_ref = bf16[11,256,640]{2,1,0:T(8,128)(2,1)} async-done(((bf16[11,64,640]{2,1,0:T(8,128)(2,1)}), bf16[11,256,640]{2,1,0:T(8,128)(2,1)}) %all-gather.3.cloned.1.call-update) | async-done | bytes 3604496 | tf_op jit(solution)/shard_map/all_gather | solution.py:115
  60.3 49.5 %all-gather.5.cloned.1.call-done.cot_ref = bf16[11,256,640]{2,1,0:T(8,128)(2,1)} async-done(((bf16[11,64,640]{2,1,0:T(8,128)(2,1)}), bf16[11,256,640]{2,1,0:T(8,128)(2,1)}) %all-gather.5.cloned.1.call-update) | async-done | bytes 3604496 | tf_op jit(solution)/shard_map/all_gather | solution.py:116
  109.8 1.1 copy-done.2
  111.0 15.5 %shard_map.137 = (bf16[11,256,640]{2,1,0:T(8,128)(2,1)}, bf16[640,1920]{1,0:T(8,128)(2,1)}) custom-call(s32[1]{0:T(128)} %min.6.live_ref, f32[11]{0:T(128)S(1)} %select_reduce_fusion.scale_ref, bf16[11,256,640]{2,1,0:T(8,128)(2,1)} %all-gather.3.cloned.1.call-done.x_ref, bf16[11,256,640]{2,1,0:T(8,128)(2,1)} %all-gather.5.cloned.1.call-done.cot_ref, ...), custom_call_target="tpu_custom_call" | custom-call | tf_op jit(solution)/shard_map/pallas_call | solution.py:74
  126.6 0.0 reduce-scatter.5.cloned.1.call-start
  126.6 0.5 reduce-scatter.5.cloned.1.call-update
  127.2 0.6 copy-done.3
  127.7 0.2 convert_reduce_fusion
  127.9 0.4 fusion.12
  128.3 65.5 %reduce-scatter.3.cloned.1.call-done = bf16[11,64,640]{2,1,0:T(8,128)(2,1)} async-done(((bf16[11,256,640]{2,1,0:T(8,128)(2,1)}), bf16[11,64,640]{2,1,0:T(8,128)(2,1)}) %reduce-scatter.3.cloned.1.call-update) | async-done | bytes 901136 | tf_op jit(solution)/shard_map/reduce_scatter | solution.py:120
  193.8 2.2 fusion.11
  196.1 1.0 fusion.10
  197.2 1.6 copy.24
  198.8 4.7 %all-to-all-start = ((bf16[11,64,640]{2,0,1:T(8,128)(2,1)}), bf16[11,64,640]{2,0,1:T(8,128)(2,1)S(1)}, u32[]{:S(2)}, u32[]{:S(2)}) async-start(bf16[11,64,640]{2,0,1:T(8,128)(2,1)} %copy.24), calls=%async_computation.1 | async-start | bytes 2621440 | tf_op jit(solution)/shard_map/all_to_all | solution.py:143
  203.5 0.1 select_reduce_fusion.1
  203.6 49.8 %all-to-all-done = bf16[11,64,640]{2,0,1:T(8,128)(2,1)S(1)} async-done(((bf16[11,64,640]{2,0,1:T(8,128)(2,1)}), bf16[11,64,640]{2,0,1:T(8,128)(2,1)S(1)}, u32[]{:S(2)}, u32[]{:S(2)}) %all-to-all-start) | async-done | bytes 901152 | tf_op jit(solution)/shard_map/all_to_all | solution.py:143
  253.5 0.2 copy.26
  253.7 0.7 gather_fusion
  254.4 1.1 broadcast_select_fusion
  255.5 3.6 %all-to-all-start.1 = ((bf16[88,8,640]{2,1,0:T(8,128)(2,1)}), bf16[88,8,640]{2,1,0:T(8,128)(2,1)S(1)}, u32[]{:S(2)}, u32[]{:S(2)}) async-start(bf16[88,8,640]{2,1,0:T(8,128)(2,1)} %broadcast_select_fusion), calls=%async_computation.2 | async-start | bytes 1802240 | tf_op jit(solution)/shard_map/all_to_all | solution.py:145
  259.1 0.0 reduce-scatter.5.cloned.1.call-done
  259.1 1.8 fusion.16
  260.9 41.2 %psum.7 = f32[640]{0:T(1024)} all-reduce(f32[640]{0:T(1024)S(1)} %get-tuple-element.9), channel_id=1, replica_groups=mesh['dp'=8,'tensor'=4] {'dp','tensor'}, use_global_device_ids=true, to_apply=%region_9.10 | all-reduce | flops 640 | bytes 5120 | tf_op jit(solution)/shard_map/psum | solution.py:137
  302.1 1.0 copy.30
  (30 shorter events, 0.1 us)
Async XLA Ops:
  7.2 3.0 copy-start.7
  7.2 1.6 copy-start.6
  7.2 1.6 copy-start.8
  7.2 1.7 copy-start.9
  7.2 102.6 %copy-start = (bf16[640,640]{1,0:T(8,128)(2,1)S(1)}, bf16[640,640]{1,0:T(8,128)(2,1)}, u32[]{:S(2)}) copy-start(bf16[640,640]{1,0:T(8,128)(2,1)} %wv_ref.1) | copy-start | bytes 2457604
  7.2 102.6 %copy-start.1 = (bf16[640,640]{1,0:T(8,128)(2,1)S(1)}, bf16[640,640]{1,0:T(8,128)(2,1)}, u32[]{:S(2)}) copy-start(bf16[640,640]{1,0:T(8,128)(2,1)} %wg_ref.1) | copy-start | bytes 2457604
  7.2 53.1 %all-gather.3.cloned.1.call-start = ((), (), s32[]{:S(2)}) async-start(), calls=%async_computation.4 | async-start | bytes 4505600 | tf_op jit(solution)/shard_map/all_gather | solution.py:115
  8.0 101.9 %all-gather.5.cloned.1.call-start = ((), (), s32[]{:S(2)}) async-start(), calls=%async_computation.5 | async-start | bytes 4505600 | tf_op jit(solution)/shard_map/all_gather | solution.py:116
  8.7 185.1 %reduce-scatter.3.cloned.1.call-start = ((), (), s32[]{:S(2)}) async-start(), calls=%async_computation.6 | async-start | bytes 4505600 | tf_op jit(solution)/shard_map/reduce_scatter | solution.py:120
  109.8 1.1 copy-start.2
  126.5 1.2 copy-start.3
  126.6 132.5 %reduce-scatter.5.cloned.1.call-start = ((), (), s32[]{:S(2)}) async-start(), calls=%async_computation.7 | async-start | bytes 2764800 | tf_op jit(solution)/shard_map/reduce_scatter | solution.py:121
  127.7 68.4 %copy-start.4 = (bf16[11,64,640]{2,1,0:T(8,128)(2,1)S(1)}, bf16[11,64,640]{2,1,0:T(8,128)(2,1)}, u32[]{:S(2)}) copy-start(bf16[11,64,640]{2,1,0:T(8,128)(2,1)} %param.11) | copy-start | bytes 2703364
  193.8 2.3 copy-start.5
  198.8 4.7 %copy-start.10 = (s32[88]{0:T(128)S(1)}, s32[88]{0:T(128)}, u32[]{:S(2)}) copy-start(s32[88]{0:T(128)} %param.14) | copy-start | bytes 1060
  198.8 54.7 %all-to-all-start = ((bf16[11,64,640]{2,0,1:T(8,128)(2,1)}), bf16[11,64,640]{2,0,1:T(8,128)(2,1)S(1)}, u32[]{:S(2)}, u32[]{:S(2)}) async-start(bf16[11,64,640]{2,0,1:T(8,128)(2,1)} %copy.24), calls=%async_computation.1 | async-start | bytes 2621440 | tf_op jit(solution)/shard_map/all_to_all | solution.py:143
  255.5 46.6 %all-to-all-start.1 = ((bf16[88,8,640]{2,1,0:T(8,128)(2,1)}), bf16[88,8,640]{2,1,0:T(8,128)(2,1)S(1)}, u32[]{:S(2)}, u32[]{:S(2)}) async-start(bf16[88,8,640]{2,1,0:T(8,128)(2,1)} %broadcast_select_fusion), calls=%async_computation.2 | async-start | bytes 1802240 | tf_op jit(solution)/shard_map/all_to_all | solution.py:145
Sparse Core Ops, SparseCore 0:
  9.9 50.3 all-gather.2
  62.1 47.6 all-gather.4
  126.7 67.1 reduce-scatter.2
  196.0 58.4 reduce-scatter.4

commit v2 on v1

v2 whole, which is shorter than its diff:
```python
import functools

import jax
import jax.numpy as jnp
import numpy as np
from jax import lax
from jax.experimental import pallas as pl
from jax.experimental.pallas import tpu as pltpu
from jax.sharding import PartitionSpec as P

eps = 1e-05


def noise_table():
    betas = np.linspace(0.00085**0.5, 0.012**0.5, 1000) ** 2
    abar = np.exp(np.cumsum(np.log1p(-betas)))
    return np.sqrt(1.0 - abar).astype(np.float32)


def block_kernel(n, ahead, scale_ref, x_ref, cot_ref, gain_ref, wv_ref, wg_ref, wo_ref,
                 ig_ref, gg_ref, dw_ref,
                 full, part, other, acc_v, acc_g, acc_o, ag_send, ag_recv, rs_send, rs_recv):
    slots, rows, width = x_ref.shape
    inner = wv_ref.shape[1]
    me = lax.axis_index("tensor")
    high = n // 2
    my_high, my_low = me // 2, me % 2
    pair = my_high * 2 + (1 - my_low)
    line = [((my_high + k) % high) * 2 + my_low for k in range(1, high)]
    peers = [(me + k) % n for k in range(1, n)]
    first = (((0,), (0,)), ((), ()))
    last = (((1,), (1,)), ((), ()))
    local = (x_ref, cot_ref)

    def send(src, dst, send_sem, recv_sem, peer):
        return pltpu.make_async_remote_copy(
            src_ref=src, dst_ref=dst, send_sem=send_sem, recv_sem=recv_sem,
            device_id={"tensor": peer}, device_id_type=pl.DeviceIdType.MESH,
        )

    def own_copies(t):
        found = []
        for peer in [pair] + line:
            for kind in (0, 1):
                found.append(send(
                    local[kind].at[t], full.at[t, kind, me],
                    ag_send.at[t, len(found)], ag_recv.at[t, kind, me], peer,
                ))
        return found

    def passed_copies(t):
        found = []
        base = 2 * high
        for peer in line:
            found.append(send(
                full.at[t, 0, pair], full.at[t, 0, pair],
                ag_send.at[t, base + len(found)], ag_recv.at[t, 0, pair], peer,
            ))
        for owner in line:
            found.append(send(
                full.at[t, 1, owner], full.at[t, 1, owner],
                ag_send.at[t, base + len(found)], ag_recv.at[t, 1, owner], pair,
            ))
        return found

    def arrived(t, kind, owner):
        send(full.at[t, kind, owner], full.at[t, kind, owner], ag_send.at[t, 0],
             ag_recv.at[t, kind, owner], pair).wait_recv()

    def sum_copies(t):
        return [
            send(part.at[t, peer], other.at[t, me], rs_send.at[t, k], rs_recv.at[t, me], peer)
            for k, peer in enumerate(peers)
        ]

    def start_own(t):
        for copy in own_copies(t):
            copy.start()

    def pass_on(t):
        for owner in [pair] + line:
            for kind in (0, 1):
                arrived(t, kind, owner)
        for copy in passed_copies(t):
            copy.start()

    barrier = pltpu.get_barrier_semaphore()
    for peer in peers:
        pl.semaphore_signal(
            barrier, inc=1, device_id={"tensor": peer}, device_id_type=pl.DeviceIdType.MESH
        )
    pl.semaphore_wait(barrier, n - 1)
    for t in range(ahead):
        start_own(t)
    acc_v[...] = jnp.zeros_like(acc_v)
    acc_g[...] = jnp.zeros_like(acc_g)
    acc_o[...] = jnp.zeros_like(acc_o)
    gg_ref[...] = jnp.zeros_like(gg_ref)
    pass_on(0)

    def one_tile(t, carry):
        @pl.when(t + ahead < slots)
        def _():
            start_own(t + ahead)

        @pl.when(t + 1 < slots)
        def _():
            pass_on(t + 1)

        full[t, 0, me] = x_ref[t]
        full[t, 1, me] = cot_ref[t]
        far = [((my_high + k) % high) * 2 + (1 - my_low) for k in range(1, high)]
        for owner in far:
            for kind in (0, 1):
                arrived(t, kind, owner)
        x = full[t, 0].reshape(n * rows, width).astype(jnp.float32)
        centred = x - jnp.mean(x, axis=-1, keepdims=True)
        inv_std = lax.rsqrt(jnp.mean(centred * centred, axis=-1, keepdims=True) + eps)
        normed = (centred * inv_std * gain_ref[...]).astype(jnp.bfloat16)
        cot = full[t, 1].reshape(n * rows, width).astype(jnp.float32)
        grad = (cot * scale_ref[t]).astype(jnp.bfloat16)
        values = jnp.dot(normed, wv_ref[...], preferred_element_type=jnp.float32)
        gate = jnp.dot(normed, wg_ref[...], preferred_element_type=jnp.float32)
        d_hidden = jnp.dot(grad, wo_ref[...], preferred_element_type=jnp.float32)
        cdf = 0.5 * (1.0 + lax.erf(gate * 0.7071067811865476))
        density = jnp.exp(-0.5 * gate * gate) * 0.3989422804014327
        gelu = gate * cdf
        hidden = (values * gelu).astype(jnp.bfloat16)
        d_value = (d_hidden * gelu).astype(jnp.bfloat16)
        d_gate = (d_hidden * values * (cdf + gate * density)).astype(jnp.bfloat16)
        d_normed = lax.dot_general(d_value, wv_ref[...], last, preferred_element_type=jnp.float32)
        d_normed += lax.dot_general(d_gate, wg_ref[...], last, preferred_element_type=jnp.float32)
        part[t] = d_normed.astype(jnp.bfloat16).reshape(n, rows, width)
        for copy in sum_copies(t):
            copy.start()
        acc_v[...] += lax.dot_general(normed, d_value, first, preferred_element_type=jnp.float32)
        acc_g[...] += lax.dot_general(normed, d_gate, first, preferred_element_type=jnp.float32)
        acc_o[...] += lax.dot_general(grad, hidden, first, preferred_element_type=jnp.float32)
        return carry

    lax.fori_loop(0, slots, one_tile, 0)
    dw_ref[:, 0:inner] = acc_v[...].astype(jnp.bfloat16)
    dw_ref[:, inner : 2 * inner] = acc_g[...].astype(jnp.bfloat16)
    dw_ref[:, 2 * inner : 3 * inner] = acc_o[...].astype(jnp.bfloat16)

    def one_norm(t, carry):
        d_normed = part[t, me].astype(jnp.float32)
        for peer in peers:
            send(part.at[t, peer], other.at[t, peer], rs_send.at[t, 0], rs_recv.at[t, peer],
                 peer).wait_recv()
            d_normed += other[t, peer].astype(jnp.float32)
        x = x_ref[t].astype(jnp.float32)
        centred = x - jnp.mean(x, axis=-1, keepdims=True)
        inv_std = lax.rsqrt(jnp.mean(centred * centred, axis=-1, keepdims=True) + eps)
        x_hat = centred * inv_std
        grad = (cot_ref[t].astype(jnp.float32) * scale_ref[t]).astype(jnp.bfloat16)
        d_hat = d_normed * gain_ref[...]
        ig_ref[t] = (grad.astype(jnp.float32) + inv_std * (
            d_hat
            - jnp.mean(d_hat, axis=-1, keepdims=True)
            - x_hat * jnp.mean(d_hat * x_hat, axis=-1, keepdims=True)
        )).astype(jnp.bfloat16)
        gg_ref[...] += jnp.sum(d_normed * x_hat, axis=0, keepdims=True)
        for copy in own_copies(t) + passed_copies(t) + sum_copies(t):
            copy.wait_send()
        return carry

    lax.fori_loop(0, slots, one_norm, 0)


def block_backward(n, scale, x, cot, gain, w_value, w_gate, w_out):
    slots, rows, width = x.shape
    inner = w_value.shape[1]
    vmem = pl.BlockSpec(memory_space=pltpu.VMEM)
    sends = 2 * n // 2 + 2 * (n // 2 - 1)
    return pl.pallas_call(
        functools.partial(block_kernel, n, min(3, slots)),
        in_specs=[pl.BlockSpec(memory_space=pltpu.SMEM)] + [vmem] * 6,
        out_specs=[vmem] * 3,
        out_shape=[
            jax.ShapeDtypeStruct((slots, rows, width), jnp.bfloat16),
            jax.ShapeDtypeStruct((1, width), jnp.float32),
            jax.ShapeDtypeStruct((width, 3 * inner), jnp.bfloat16),
        ],
        scratch_shapes=[
            pltpu.VMEM((slots, 2, n, rows, width), jnp.bfloat16),
            pltpu.VMEM((slots, n, rows, width), jnp.bfloat16),
            pltpu.VMEM((slots, n, rows, width), jnp.bfloat16),
        ]
        + [pltpu.VMEM((width, inner), jnp.float32)] * 3
        + [
            pltpu.SemaphoreType.DMA((slots, sends)),
            pltpu.SemaphoreType.DMA((slots, 2, n)),
            pltpu.SemaphoreType.DMA((slots, n)),
            pltpu.SemaphoreType.DMA((slots, n)),
        ],
        compiler_params=pltpu.CompilerParams(
            collective_id=0, has_side_effects=True, vmem_limit_bytes=52 * 1024 * 1024
        ),
    )(scale, x, cot, gain, w_value, w_gate, w_out)


def per_device(latents, cotangent, trunc_steps, timesteps, tile_map, gain, w_value, w_gate, w_out):
    slots, local_rows, width = latents.shape
    total = tile_map.shape[0]
    inner = w_value.shape[1]
    me = lax.axis_index("dp")
    live = jnp.clip(lax.dynamic_index_in_dim(trunc_steps, me, 0, keepdims=True) - 29, 1, slots)
    times = lax.dynamic_slice_in_dim(timesteps, me * slots, slots, 0)
    table = jnp.asarray(noise_table())
    scale = jnp.sum(
        jnp.where(times[:, None] == jnp.arange(1000, dtype=jnp.int32)[None, :], table[None, :], 0.0),
        axis=1,
    )
    scale = jnp.where(jnp.arange(slots, dtype=jnp.int32) < live[0], scale, 0.0)
    input_grad, gain_part, dw_part = block_backward(
        lax.axis_size("tensor"), scale, latents, cotangent, gain[None, :], w_value, w_gate, w_out
    )
    grad_gain = lax.psum(gain_part[0], ("dp", "tensor"))
    dw = lax.psum_scatter(dw_part, "dp", scatter_dimension=0, tiled=True).astype(jnp.float32)

    item_ids = jnp.arange(total, dtype=jnp.int32)
    source = jnp.sum(
        jnp.where(tile_map[:, None] == item_ids[None, :], item_ids[:, None], 0), axis=0
    )
    pieces = lax.all_to_all(input_grad, "dp", split_axis=1, concat_axis=0, tiled=True)
    pieces = jnp.take(pieces, source, axis=0)
    placed = lax.all_to_all(pieces, "dp", split_axis=0, concat_axis=1, tiled=True)
    return (
        placed,
        dw[:, :inner],
        dw[:, inner : 2 * inner],
        dw[:, 2 * inner :],
        grad_gain,
    )


def solution(mesh):
    in_specs = (
        P("dp", "tensor", None),
        P("dp", "tensor", None),
        P(),
        P(),
        P(),
        P(),
        P(None, "tensor"),
        P(None, "tensor"),
        P(None, "tensor"),
    )
    out_specs = (
        P("dp", "tensor", None),
        P("dp", "tensor"),
        P("dp", "tensor"),
        P("dp", "tensor"),
        P(),
    )
    return jax.shard_map(
        per_device, mesh=mesh, in_specs=in_specs, out_specs=out_specs, check_vma=False
    )
```

time: 308 us -> 240 us (0.78)
  waiting for transfers between devices: 217 us -> 50 us
  Pallas kernels: 15.5 us -> 109 us
  local copies, waits for them, and re-layouts: 7.81 us -> 11.5 us
  other arithmetic: 5.28 us -> 2.13 us
    all_gather x2 -> x0, waiting for transfers between devices: 99.5 us -> none  [the longest x1 50 us: per_device(): full_x = lax.all_gather(latents, 'tensor', axis=1, tiled=True)]
    pallas_call x1, Pallas kernels: 15.5 us -> 109 us  [block_backward(): pl.pallas_call(functools.partial(block_kernel, n, min(3, slots)), in_spec...]
    reduce_scatter x1 -> x0, waiting for transfers between devices: 65.5 us -> none  [per_device(): lax.psum_scatter(dn_part, 'tensor', scatter_dimension=1, tiled=True)]
  transfers between devices with their start and end apart: 6 -> 3, of which waited for: 4 -> 1; matrix products, arithmetic and copies ran while one was open for 3% -> 2% of each run, Pallas kernels for 0% -> 0%
where the time goes in v2:
time: 240 us
  Pallas kernels  109 us (45%)
  waiting for transfers between devices  50 us (21%)
  blocking collectives  43.2 us (18%)
  between operations  14.8 us (6%)
  local copies, waits for them, and re-layouts  11.5 us (5%)
  starting transfers between devices  8.6 us (4%)
    pallas_call x1, Pallas kernels, block_backward(): pl.pallas_call(functools.partial(block_kernel, n, min(3, slots)), in_spec...  109 us
    all_to_all x1, waiting for transfers between devices, per_device(): lax.all_to_all(input_grad, 'dp', split_axis=1, concat_axis=0, tiled=True)  50 us
    psum x1, blocking collectives, per_device(): grad_gain = lax.psum(gain_part[0], ('dp', 'tensor'))  43.2 us
    all_to_all x1, starting transfers between devices, per_device(): lax.all_to_all(input_grad, 'dp', split_axis=1, concat_axis=0, tiled=True)  5.01 us
  transfers between devices with their start and end apart: 3, of which 1 were waited for; matrix products, arithmetic and copies ran while one was open for 2% of the time, Pallas kernels for 0%

profile of v2, /device:TPU:0, one launch (start us, length us, event | category | flops | bytes accessed | tf_op | source)
XLA Modules:
  0.0 239.6 jit_solution(6745654433828585738)
XLA Ops:
  7.2 0.0 reduce-scatter.2.cloned.1.call-start
  7.2 0.7 broadcast_in_dim.53.gain_ref
  7.9 0.7 dynamic_slice.8
  8.6 1.2 dynamic_slice.7
  10.5 0.9 select_reduce_fusion
  11.4 0.0 copy-start
  11.4 1.1 copy-done
  12.6 0.0 copy-start.1
  12.6 1.1 copy-done.1
  13.7 109.4 %shard_map.137 = (bf16[11,64,640]{2,1,0:T(8,128)(2,1)}, f32[1,640]{1,0:T(1,128)S(1)}, bf16[640,1920]{1,0:T(8,128)(2,1)}) custom-call(f32[11]{0:T(128)S(1)} %compare_select_fusion.2.scale_ref, bf16[11,64,640]{2,1,0:T(8,128)(2,1)} %x_ref.1, bf16[11,64,640]{2,1,0:T(8,128)(2,1)} %cot_ref.1, f32[1,640]{1,0:T(1,128)S(1)} %broadcast_in_dim.53.gain_ref, ...), custom_call_target="tpu_custom_call" | custom-call | tf_op jit(solution)/shard_map/pallas_call | solution.py:176
  123.1 0.0 copy-start.2
  123.1 0.0 reduce-scatter.2.cloned.1.call-update
  123.1 1.1 copy-done.2
  124.3 1.6 copy.24
  125.9 0.0 copy-start.3
  125.9 5.0 %all-to-all-start = ((bf16[11,64,640]{2,0,1:T(8,128)(2,1)}), bf16[11,64,640]{2,0,1:T(8,128)(2,1)S(1)}, u32[]{:S(2)}, u32[]{:S(2)}) async-start(bf16[11,64,640]{2,0,1:T(8,128)(2,1)} %copy.24), calls=%async_computation | async-start | bytes 2621440 | tf_op jit(solution)/shard_map/all_to_all | solution.py:226
  130.9 0.0 copy-done.3
  130.9 0.1 select_reduce_fusion.1
  131.0 50.0 %all-to-all-done = bf16[11,64,640]{2,0,1:T(8,128)(2,1)S(1)} async-done(((bf16[11,64,640]{2,0,1:T(8,128)(2,1)}), bf16[11,64,640]{2,0,1:T(8,128)(2,1)S(1)}, u32[]{:S(2)}, u32[]{:S(2)}) %all-to-all-start) | async-done | bytes 901152 | tf_op jit(solution)/shard_map/all_to_all | solution.py:226
  181.0 0.2 copy.26
  181.2 0.7 gather_fusion
  182.0 1.1 broadcast_select_fusion
  183.1 3.6 %all-to-all-start.1 = ((bf16[88,8,640]{2,1,0:T(8,128)(2,1)}), bf16[88,8,640]{2,1,0:T(8,128)(2,1)S(1)}, u32[]{:S(2)}, u32[]{:S(2)}) async-start(bf16[88,8,640]{2,1,0:T(8,128)(2,1)} %broadcast_select_fusion), calls=%async_computation.1 | async-start | bytes 1802240 | tf_op jit(solution)/shard_map/all_to_all | solution.py:228
  186.7 43.2 %psum.7 = f32[640]{0:T(1024)} all-reduce(f32[640]{0:T(1024)S(1)} %reduce), channel_id=1, replica_groups=mesh['dp'=8,'tensor'=4] {'dp','tensor'}, use_global_device_ids=true, to_apply=%region_3.4 | all-reduce | flops 640 | bytes 5120 | tf_op jit(solution)/shard_map/psum | solution.py:219
  229.9 0.0 all-to-all-done.1
  229.9 1.0 copy.30
  230.9 0.0 reduce-scatter.2.cloned.1.call-done
  230.9 1.8 fusion.1
  (5 shorter events, 0.0 us)
Async XLA Ops:
  7.2 223.7 %reduce-scatter.2.cloned.1.call-start = ((), (), s32[]{:S(2)}) async-start(), calls=%async_computation.3 | async-start | bytes 2764800 | tf_op jit(solution)/shard_map/reduce_scatter | solution.py:220
  11.4 1.1 copy-start
  12.6 1.1 copy-start.1
  123.1 1.2 copy-start.2
  125.9 5.0 %copy-start.3 = (s32[88]{0:T(128)S(1)}, s32[88]{0:T(128)}, u32[]{:S(2)}) copy-start(s32[88]{0:T(128)} %param.14) | copy-start | bytes 1060
  125.9 55.2 %all-to-all-start = ((bf16[11,64,640]{2,0,1:T(8,128)(2,1)}), bf16[11,64,640]{2,0,1:T(8,128)(2,1)S(1)}, u32[]{:S(2)}, u32[]{:S(2)}) async-start(bf16[11,64,640]{2,0,1:T(8,128)(2,1)} %copy.24), calls=%async_computation | async-start | bytes 2621440 | tf_op jit(solution)/shard_map/all_to_all | solution.py:226
  183.1 46.8 %all-to-all-start.1 = ((bf16[88,8,640]{2,1,0:T(8,128)(2,1)}), bf16[88,8,640]{2,1,0:T(8,128)(2,1)S(1)}, u32[]{:S(2)}, u32[]{:S(2)}) async-start(bf16[88,8,640]{2,1,0:T(8,128)(2,1)} %broadcast_select_fusion), calls=%async_computation.1 | async-start | bytes 1802240 | tf_op jit(solution)/shard_map/all_to_all | solution.py:228
Sparse Core Ops, SparseCore 0:
  123.2 59.4 reduce-scatter.1

commit v3 on v2

--- a/solution.py
+++ b/solution.py
@@ -17,9 +17,13 @@
     return np.sqrt(1.0 - abar).astype(np.float32)
 
 
-def block_kernel(n, ahead, scale_ref, x_ref, cot_ref, gain_ref, wv_ref, wg_ref, wo_ref,
-                 ig_ref, gg_ref, dw_ref,
-                 full, part, other, acc_v, acc_g, acc_o, ag_send, ag_recv, rs_send, rs_recv):
+def block_kernel(n, groups, ahead, lag, late, scale_ref, source_ref, x_ref, cot_ref, gain_ref,
+                 wv_ref, wg_ref, wo_ref, ig_ref, gg_ref, dv_ref, dg_ref, do_ref,
+                 full, part, other, acc_v, acc_g, acc_o, placed, gain_one, gain_two,
+                 dw_part, dw_pair, dw_sum, dw_other,
+                 ag_send, ag_recv, rs_send, rs_recv, out_send, out_recv,
+                 gain_send, gain_recv, far_send, far_recv,
+                 pair_send, pair_recv, sum_send, sum_recv):
     slots, rows, width = x_ref.shape
     inner = wv_ref.shape[1]
     me = lax.axis_index("tensor")
@@ -31,6 +35,34 @@
     first = (((0,), (0,)), ((), ()))
     last = (((1,), (1,)), ((), ()))
     local = (x_ref, cot_ref)
+    group = lax.axis_index("dp")
+    chips = groups // 2
+    chip, core = group // 2, group % 2
+    twin = chip * 2 + (1 - core)
+    away = [((chip + k) % chips) for k in range(1, chips)]
+    block = dw_part.shape[1]
+
+    def cross(src, dst, send_sem, recv_sem, peer):
+        return pltpu.make_async_remote_copy(
+            src_ref=src, dst_ref=dst, send_sem=send_sem, recv_sem=recv_sem,
+            device_id={"dp": peer}, device_id_type=pl.DeviceIdType.MESH,
+        )
+
+    def out_copy(t, owner, index, peer):
+        spot = placed.at[owner * slots + t]
+        return cross(spot, spot, out_send.at[t, index], out_recv.at[t, owner], peer)
+
+    def out_own(t):
+        found = [out_copy(t, group, k, c * 2 + core) for k, c in enumerate(away)]
+        return found + [out_copy(t, group, chips - 1, twin)]
+
+    def out_passed(t):
+        return [out_copy(t, c * 2 + core, chips + k, twin) for k, c in enumerate(away)]
+
+    def pass_out(t):
+        for c, copy in zip(away, out_passed(t), strict=True):
+            out_copy(t, c * 2 + core, 0, twin).wait_recv()
+            copy.start()
 
     def send(src, dst, send_sem, recv_sem, peer):
         return pltpu.make_async_remote_copy(
@@ -89,7 +121,12 @@
         pl.semaphore_signal(
             barrier, inc=1, device_id={"tensor": peer}, device_id_type=pl.DeviceIdType.MESH
         )
-    pl.semaphore_wait(barrier, n - 1)
+    for k in range(1, groups):
+        pl.semaphore_signal(
+            barrier, inc=1, device_id={"dp": (group + k) % groups},
+            device_id_type=pl.DeviceIdType.MESH,
+        )
+    pl.semaphore_wait(barrier, n - 1 + groups - 1)
     for t in range(ahead):
         start_own(t)
     acc_v[...] = jnp.zeros_like(acc_v)
@@ -97,6 +134,27 @@
     acc_o[...] = jnp.zeros_like(acc_o)
     gg_ref[...] = jnp.zeros_like(gg_ref)
     pass_on(0)
+
+    def finish(t):
+        d_normed = part[t, me].astype(jnp.float32)
+        for peer in peers:
+            send(part.at[t, peer], other.at[t, peer], rs_send.at[t, 0], rs_recv.at[t, peer],
+                 peer).wait_recv()
+            d_normed += other[t, peer].astype(jnp.float32)
+        x = x_ref[t].astype(jnp.float32)
+        centred = x - jnp.mean(x, axis=-1, keepdims=True)
+        inv_std = lax.rsqrt(jnp.mean(centred * centred, axis=-1, keepdims=True) + eps)
+        x_hat = centred * inv_std
+        grad = (cot_ref[t].astype(jnp.float32) * scale_ref[t]).astype(jnp.bfloat16)
+        d_hat = d_normed * gain_ref[...]
+        placed[group * slots + t] = (grad.astype(jnp.float32) + inv_std * (
+            d_hat
+            - jnp.mean(d_hat, axis=-1, keepdims=True)
+            - x_hat * jnp.mean(d_hat * x_hat, axis=-1, keepdims=True)
+        )).astype(jnp.bfloat16)
+        for copy in out_own(t):
+            copy.start()
+        gg_ref[...] += jnp.sum(d_normed * x_hat, axis=0, keepdims=True)
 
     def one_tile(t, carry):
         @pl.when(t + ahead < slots)
@@ -136,51 +194,128 @@
         acc_v[...] += lax.dot_general(normed, d_value, first, preferred_element_type=jnp.float32)
         acc_g[...] += lax.dot_general(normed, d_gate, first, preferred_element_type=jnp.float32)
         acc_o[...] += lax.dot_general(grad, hidden, first, preferred_element_type=jnp.float32)
+
+        @pl.when(t >= lag)
+        def _():
+            finish(t - lag)
+
+        @pl.when(t >= lag + late)
+        def _():
+            pass_out(t - lag - late)
+
         return carry
 
     lax.fori_loop(0, slots, one_tile, 0)
-    dw_ref[:, 0:inner] = acc_v[...].astype(jnp.bfloat16)
-    dw_ref[:, inner : 2 * inner] = acc_g[...].astype(jnp.bfloat16)
-    dw_ref[:, 2 * inner : 3 * inner] = acc_o[...].astype(jnp.bfloat16)
-
-    def one_norm(t, carry):
-        d_normed = part[t, me].astype(jnp.float32)
-        for peer in peers:
-            send(part.at[t, peer], other.at[t, peer], rs_send.at[t, 0], rs_recv.at[t, peer],
-                 peer).wait_recv()
-            d_normed += other[t, peer].astype(jnp.float32)
-        x = x_ref[t].astype(jnp.float32)
-        centred = x - jnp.mean(x, axis=-1, keepdims=True)
-        inv_std = lax.rsqrt(jnp.mean(centred * centred, axis=-1, keepdims=True) + eps)
-        x_hat = centred * inv_std
-        grad = (cot_ref[t].astype(jnp.float32) * scale_ref[t]).astype(jnp.bfloat16)
-        d_hat = d_normed * gain_ref[...]
-        ig_ref[t] = (grad.astype(jnp.float32) + inv_std * (
-            d_hat
-            - jnp.mean(d_hat, axis=-1, keepdims=True)
-            - x_hat * jnp.mean(d_hat * x_hat, axis=-1, keepdims=True)
-        )).astype(jnp.bfloat16)
-        gg_ref[...] += jnp.sum(d_normed * x_hat, axis=0, keepdims=True)
-        for copy in own_copies(t) + passed_copies(t) + sum_copies(t):
+    for d in range(groups):
+        rows_of = slice(d * block, (d + 1) * block)
+        for k, acc in enumerate((acc_v, acc_g, acc_o)):
+            dw_part[d, :, k * inner : (k + 1) * inner] = acc[rows_of, :].astype(jnp.bfloat16)
+    pair_copies = [
+        cross(dw_part.at[c * 2 + 1 - core], dw_pair.at[c], pair_send.at[c], pair_recv.at[c], twin)
+        for c in range(chips)
+    ]
+    for copy in pair_copies:
+        copy.start()
+
+    def drain(t, carry):
+        finish(t)
+        return carry
+
+    lax.fori_loop(slots - lag, slots, drain, 0)
+    gain_one[me] = gg_ref[...]
+    gain_copies = [
+        send(gg_ref, gain_one.at[me], gain_send.at[k], gain_recv.at[me], peer)
+        for k, peer in enumerate(peers)
+    ]
+    for copy in gain_copies:
+        copy.start()
+    for copy in pair_copies:
+        copy.wait()
+    for c in range(chips):
+        both = dw_part[c * 2 + core].astype(jnp.float32) + dw_pair[c].astype(jnp.float32)
+        dw_sum[c] = both.astype(jnp.bfloat16)
+    sum_copies_z = [
+        cross(dw_sum.at[c], dw_other.at[chip], sum_send.at[k], sum_recv.at[chip], c * 2 + core)
+        for k, c in enumerate(away)
+    ]
+    for copy in sum_copies_z:
+        copy.start()
+
+    def drain_out(t, carry):
+        pass_out(t)
+        return carry
+
+    lax.fori_loop(slots - lag - late, slots, drain_out, 0)
+    for peer in peers:
+        send(gg_ref, gain_one.at[peer], gain_send.at[0], gain_recv.at[peer], peer).wait_recv()
+    for copy in gain_copies:
+        copy.wait_send()
+    gain_sum = gain_one[0]
+    for k in range(1, n):
+        gain_sum += gain_one[k]
+    gain_two[group] = gain_sum
+    far_copies = [
+        cross(gain_two.at[group], gain_two.at[group], far_send.at[k], far_recv.at[group],
+              (group + k) % groups)
+        for k in range(1, groups)
+    ]
+    for copy in far_copies:
+        copy.start()
+
+    def settle(t, carry):
+        for c in range(chips):
+            out_copy(t, c * 2 + 1 - core, 0, twin).wait_recv()
+        for copy in own_copies(t) + passed_copies(t) + sum_copies(t) + out_own(t) + out_passed(t):
             copy.wait_send()
         return carry
 
-    lax.fori_loop(0, slots, one_norm, 0)
-
-
-def block_backward(n, scale, x, cot, gain, w_value, w_gate, w_out):
+    lax.fori_loop(0, slots, settle, 0)
+
+    def place(t, carry):
+        ig_ref[t] = placed[source_ref[t]]
+        return carry
+
+    lax.fori_loop(0, slots, place, 0)
+    for k in range(1, groups):
+        peer = (group + k) % groups
+        cross(gain_two.at[peer], gain_two.at[peer], far_send.at[k], far_recv.at[peer],
+              peer).wait_recv()
+    for copy in far_copies:
+        copy.wait_send()
+    gain_total = gain_two[0]
+    for k in range(1, groups):
+        gain_total += gain_two[k]
+    gg_ref[...] = gain_total
+    result = dw_sum[chip].astype(jnp.float32)
+    for c in away:
+        cross(dw_other.at[c], dw_other.at[c], sum_send.at[0], sum_recv.at[c], twin).wait_recv()
+        result += dw_other[c].astype(jnp.float32)
+    for copy in sum_copies_z:
+        copy.wait_send()
+    dv_ref[...] = result[:, 0:inner]
+    dg_ref[...] = result[:, inner : 2 * inner]
+    do_ref[...] = result[:, 2 * inner : 3 * inner]
+
+
+def block_backward(n, groups, scale, source, x, cot, gain, w_value, w_gate, w_out):
     slots, rows, width = x.shape
     inner = w_value.shape[1]
+    chips = groups // 2
+    block = width // groups
     vmem = pl.BlockSpec(memory_space=pltpu.VMEM)
-    sends = 2 * n // 2 + 2 * (n // 2 - 1)
+    smem = pl.BlockSpec(memory_space=pltpu.SMEM)
+    grads = jax.ShapeDtypeStruct((block, inner), jnp.float32)
+    dma = pltpu.SemaphoreType.DMA
     return pl.pallas_call(
-        functools.partial(block_kernel, n, min(3, slots)),
-        in_specs=[pl.BlockSpec(memory_space=pltpu.SMEM)] + [vmem] * 6,
-        out_specs=[vmem] * 3,
+        functools.partial(block_kernel, n, groups, 3, 2, 2),
+        in_specs=[smem] * 2 + [vmem] * 6,
+        out_specs=[vmem] * 5,
         out_shape=[
             jax.ShapeDtypeStruct((slots, rows, width), jnp.bfloat16),
             jax.ShapeDtypeStruct((1, width), jnp.float32),
-            jax.ShapeDtypeStruct((width, 3 * inner), jnp.bfloat16),
+            grads,
+            grads,
+            grads,
         ],
         scratch_shapes=[
             pltpu.VMEM((slots, 2, n, rows, width), jnp.bfloat16),
@@ -189,15 +324,32 @@
         ]
         + [pltpu.VMEM((width, inner), jnp.float32)] * 3
         + [
-            pltpu.SemaphoreType.DMA((slots, sends)),
-            pltpu.SemaphoreType.DMA((slots, 2, n)),
-            pltpu.SemaphoreType.DMA((slots, n)),
-            pltpu.SemaphoreType.DMA((slots, n)),
+            pltpu.VMEM((groups * slots, rows, width), jnp.bfloat16),
+            pltpu.VMEM((n, 1, width), jnp.float32),
+            pltpu.VMEM((groups, 1, width), jnp.float32),
+            pltpu.VMEM((groups, block, 3 * inner), jnp.bfloat16),
+            pltpu.VMEM((chips, block, 3 * inner), jnp.bfloat16),
+            pltpu.VMEM((chips, block, 3 * inner), jnp.bfloat16),
+            pltpu.VMEM((chips, block, 3 * inner), jnp.bfloat16),
+            dma((slots, n + 2 * (n // 2 - 1))),
+            dma((slots, 2, n)),
+            dma((slots, n)),
+            dma((slots, n)),
+            dma((slots, 2 * chips - 1)),
+            dma((slots, groups)),
+            dma((n,)),
+            dma((n,)),
+            dma((groups,)),
+            dma((groups,)),
+            dma((chips,)),
+            dma((chips,)),
+            dma((chips,)),
+            dma((chips,)),
         ],
         compiler_params=pltpu.CompilerParams(
-            collective_id=0, has_side_effects=True, vmem_limit_bytes=52 * 1024 * 1024
+            collective_id=0, has_side_effects=True, vmem_limit_bytes=60 * 1024 * 1024
         ),
-    )(scale, x, cot, gain, w_value, w_gate, w_out)
+    )(scale, source, x, cot, gain, w_value, w_gate, w_out)
 
 
 def per_device(latents, cotangent, trunc_steps, timesteps, tile_map, gain, w_value, w_gate, w_out):
@@ -213,26 +365,16 @@
         axis=1,
     )
     scale = jnp.where(jnp.arange(slots, dtype=jnp.int32) < live[0], scale, 0.0)
-    input_grad, gain_part, dw_part = block_backward(
-        lax.axis_size("tensor"), scale, latents, cotangent, gain[None, :], w_value, w_gate, w_out
-    )
-    grad_gain = lax.psum(gain_part[0], ("dp", "tensor"))
-    dw = lax.psum_scatter(dw_part, "dp", scatter_dimension=0, tiled=True).astype(jnp.float32)
-
     item_ids = jnp.arange(total, dtype=jnp.int32)
+    my_slots = me * slots + jnp.arange(slots, dtype=jnp.int32)
     source = jnp.sum(
-        jnp.where(tile_map[:, None] == item_ids[None, :], item_ids[:, None], 0), axis=0
-    )
-    pieces = lax.all_to_all(input_grad, "dp", split_axis=1, concat_axis=0, tiled=True)
-    pieces = jnp.take(pieces, source, axis=0)
-    placed = lax.all_to_all(pieces, "dp", split_axis=0, concat_axis=1, tiled=True)
-    return (
-        placed,
-        dw[:, :inner],
-        dw[:, inner : 2 * inner],
-        dw[:, 2 * inner :],
-        grad_gain,
-    )
+        jnp.where(tile_map[:, None] == my_slots[None, :], item_ids[:, None], 0), axis=0
+    )
+    placed, grad_gain, grad_value, grad_gate, grad_out_proj = block_backward(
+        lax.axis_size("tensor"), lax.axis_size("dp"), scale, source, latents, cotangent,
+        gain[None, :], w_value, w_gate, w_out,
+    )
+    return (placed, grad_value, grad_gate, grad_out_proj, grad_gain[0])
 
 
 def solution(mesh):

time: 240 us -> 172 us (0.72)
  Pallas kernels: 109 us -> 160 us
  waiting for transfers between devices: 50 us -> 0 us
  blocking collectives: 43.2 us -> 0 us
  between operations: 14.8 us -> 1.37 us
  starting transfers between devices: 8.6 us -> 0 us
  local copies, waits for them, and re-layouts: 11.5 us -> 8.03 us
    pallas_call x1, Pallas kernels: 109 us -> 160 us  [block_backward(): pl.pallas_call(functools.partial(block_kernel, n, groups, 3, 2, 2), in_sp...]
    all_to_all x2 -> x0, waiting for transfers between devices: 50 us -> none  [the longest x1 50 us: per_device(): lax.all_to_all(input_grad, 'dp', split_axis=1, concat_axis=0, tiled=True)]
    psum x1 -> x0, blocking collectives: 43.2 us -> none  [per_device(): grad_gain = lax.psum(gain_part[0], ('dp', 'tensor'))]
    all_to_all x2 -> x0, starting transfers between devices: 8.56 us -> none  [the longest x1 5.01 us: per_device(): lax.all_to_all(input_grad, 'dp', split_axis=1, concat_axis=0, tiled=True)]
    unnamed x8 -> x22, local copies, waits for them, and re-layouts: 3.43 us -> 6.79 us
  transfers between devices with their start and end apart: 3 -> 0, of which waited for: 1 -> 0; matrix products, arithmetic and copies ran while one was open for 2% -> 0% of each run, Pallas kernels for 0% -> 0%
where the time goes in v3:
time: 172 us; the launch traced here: 171 us
  Pallas kernels  160 us (93%)
  local copies, waits for them, and re-layouts  8.03 us (5%)
  other arithmetic  2.01 us (1%)
    pallas_call x1, Pallas kernels, block_backward(): pl.pallas_call(functools.partial(block_kernel, n, groups, 3, 2, 2), in_sp...  160 us
    unnamed x22, local copies, waits for them, and re-layouts  6.79 us

profile of v3, /device:TPU:0, one launch (start us, length us, event | category | flops | bytes accessed | tf_op | source)
XLA Modules:
  0.0 171.4 jit_solution(4000746859027358158)
XLA Ops:
  0.6 0.0 copy-start.6
  0.7 0.6 copy-done.6
  1.3 0.0 copy-start.7
  1.3 0.7 select_reduce_fusion.1.source_ref
  2.0 0.0 copy-done.7
  2.0 0.0 copy-start.8
  2.0 0.1 dynamic_slice.8
  2.1 0.6 copy-done.8
  2.6 0.6 dynamic_slice.7
  3.2 0.0 copy-start.3
  3.9 0.0 copy-start.4
  3.9 0.0 copy-done.3
  3.9 0.2 select_reduce_fusion
  4.1 0.5 compare_select_fusion.scale_ref
  4.6 0.0 copy-done.4
  4.6 0.6 broadcast_in_dim.42.gain_ref
  5.2 160.0 %shard_map.137 = (bf16[11,64,640]{2,1,0:T(8,128)(2,1)}, f32[1,640]{1,0:T(1,128)}, f32[80,640]{1,0:T(8,128)}, f32[80,640]{1,0:T(8,128)}, f32[80,640]{1,0:T(8,128)}) custom-call(f32[11]{0:T(128)} %compare_select_fusion.scale_ref, s32[11]{0:T(128)} %select_reduce_fusion.1.source_ref, bf16[11,64,640]{2,1,0:T(8,128)(2,1)} %x_ref.1, bf16[11,64,640]{2,1,0:T(8,128)(2,1)} %cot_ref.1, ...), custom_call_target="tpu_custom_call" | custom-call | tf_op jit(solution)/shard_map/pallas_call | solution.py:309
  165.3 0.0 copy-start.5
  165.3 0.7 copy-done.5
  165.9 0.6 reduce
  166.5 0.0 copy-start.2
  166.5 2.2 %copy.19 = bf16[11,64,640]{2,1,0:T(8,128)(2,1)} copy(bf16[11,64,640]{2,1,0:T(8,128)(2,1)} %get-tuple-element.20) | data formatting | bytes 1802240
  168.7 0.0 copy-done.2
  168.7 0.0 copy-start.1
  168.7 0.7 copy.20
  169.4 0.3 copy-done.1
  169.8 0.0 copy-start
  169.8 0.7 copy.21
  170.4 0.3 copy-done
  170.8 0.7 copy.22
  (1 shorter events, 0.0 us)
Async XLA Ops:
  0.6 0.7 copy-start.6
  1.3 0.7 copy-start.7
  2.0 0.7 copy-start.8
  3.2 0.7 copy-start.3
  3.9 0.7 copy-start.4
  165.3 0.7 copy-start.5
  166.5 2.2 %copy-start.2 = (f32[80,640]{1,0:T(8,128)S(1)}, f32[80,640]{1,0:T(8,128)}, u32[]{:S(2)}) copy-start(f32[80,640]{1,0:T(8,128)} %get-tuple-element.21) | copy-start | bytes 614404
  168.7 1.0 copy-start.1
  169.8 1.0 copy-start
